TPU v7x, 32 devices: a whole 2x2x4 slice. The times are simulated.
32 devices in a mesh: rep: 16 (over z, y, core), tp: 2 (over x).
Axes of the slice: x: 2, y: 2, z: 4, core: 2. Of those that a mesh axis runs over, the one named last changes fastest.
Arguments:
- positions: int32 [4096], P('rep'), may hold values from 0 to 8191
- activations: bfloat16 [4096, 4096], P('rep', 'tp'), may hold values from -6 to 6
- norm_gain: bfloat16 [4096], P('tp'), may hold values from 0.5 to 1.5
- qkv_weight: bfloat16 [4096, 6144], P('rep', 'tp'), may hold values from -0.09375 to 0.09375
- gate_up_weight: bfloat16 [4096, 14336], P('rep', 'tp'), may hold values from -0.09375 to 0.09375
Outputs:
- qkv_out: bfloat16 [4096, 6144], P('rep', 'tp')
- hidden: bfloat16 [4096, 7168], P('rep', 'tp')
All inputs are finite; a program needn't handle non-finite values.
Results may differ from a plain program's by a relative error of at most 0.0058.
Values may be sent and summed in bfloat16 or wider, within the bound.
A program may use at most 192 MiB of HBM per device.

v0:
```python
import jax
import jax.numpy as jnp
from jax import lax
from jax.sharding import PartitionSpec as P

QH = 32
KVH = 8
HD = 128


theta_base = 500000.0
norm_eps = 1e-05


def normalize(gathered, gain_row):
    values = gathered.astype(jnp.float32)
    mean_square = jnp.mean(values * values, axis=1, keepdims=True)
    return (values * lax.rsqrt(mean_square + norm_eps) * gain_row.astype(jnp.float32)).astype(
        jnp.bfloat16
    )


def rotary(joined_qkv, positions):
    row_count = joined_qkv.shape[0]
    per_group = QH // KVH + 2
    half_size = HD // 2
    head_view = joined_qkv.reshape(row_count, -1, per_group, HD)
    frequency = theta_base ** (-2.0 * jnp.arange(half_size, dtype=jnp.float32) / HD)
    angles = positions.astype(jnp.float32)[:, None] * frequency[None, :]
    cosine = jnp.cos(angles)[:, None, None, :]
    sine_part = jnp.sin(angles)[:, None, None, :]
    leading = head_view[..., :half_size]
    trailing = head_view[..., half_size:]
    turned = jnp.concatenate(
        [leading * cosine - trailing * sine_part, trailing * cosine + leading * sine_part], axis=-1
    )
    rotated_mask = (jnp.arange(per_group) < per_group - 1)[None, None, :, None]
    return jnp.where(rotated_mask, turned, head_view).reshape(row_count, -1)


def contract_rows(chosen, piece):
    return jnp.dot(chosen, piece, preferred_element_type=jnp.float32)


def per_device(positions, activations, norm_gain, qkv_weight, gate_up_weight):
    features, gains = (
        lax.all_gather(activations, "tp", axis=1, tiled=True),
        lax.all_gather(norm_gain, "tp", axis=0, tiled=True),
    )
    normed = normalize(features, gains)
    seq_count = normed.shape[0]
    qkv_partial = contract_rows(normed, lax.all_gather(qkv_weight, "rep", axis=0, tiled=True))
    gateup_partial = contract_rows(
        normed, lax.all_gather(gate_up_weight, "rep", axis=0, tiled=True)
    )
    qkv_out = rotary(qkv_partial, positions).astype(jnp.bfloat16)
    paired = gateup_partial.reshape(seq_count, 2, -1)
    hidden = (jax.nn.silu(paired[:, 0]) * paired[:, 1]).astype(jnp.bfloat16)
    return (qkv_out, hidden)


def solution(mesh):
    placed = (P("rep"), P("rep", "tp"), P("tp"), P("rep", "tp"), P("rep", "tp"))
    return jax.shard_map(
        per_device,
        mesh=mesh,
        in_specs=placed,
        out_specs=(P("rep", "tp"), P("rep", "tp")),
        check_vma=False,
    )
```

profile of v0, /device:TPU:0, one launch (start us, length us, event | category | flops | bytes accessed | tf_op | source)
XLA Modules:
  0.0 519.1 jit_solution(3745872662002425558)
XLA Ops:
  7.2 0.0 copy-start
  7.2 0.0 all-gather.4.cloned.1.call-start
  7.2 0.7 all-gather.4.cloned.1.call-update
  7.9 0.0 all-gather.6.cloned.1.call-start
  8.0 0.7 all-gather.6.cloned.1.call-update
  8.7 0.0 all-gather.8.cloned.1.call-start
  8.7 0.7 all-gather.8.cloned.1.call-update
  9.4 5.3 %all_gather.13 = bf16[4096]{0:T(1024)(128)(2,1)S(1)} all-gather(bf16[2048]{0:T(1024)(128)(2,1)S(1)} %copy-done), channel_id=1, replica_groups=mesh['rep'=16,'tp'=2] {'tp'}, dimensions={0}, use_global_device_ids=true | all-gather | bytes 12288 | tf_op jit(solution)/shard_map/all_gather | solution.py:48
  14.7 0.1 broadcast_in_dim.9
  14.8 0.3 multiply_cosine_fusion
  15.1 30.2 %all-gather.4.cloned.1.call-done = bf16[256,4096]{1,0:T(8,128)(2,1)} async-done(((bf16[256,2048]{1,0:T(8,128)(2,1)}), bf16[256,4096]{1,0:T(8,128)(2,1)}) %all-gather.4.cloned.1.call-update) | async-done | bytes 2097168 | tf_op jit(solution)/shard_map/all_gather | solution.py:47
  45.4 2.1 fusion
  47.5 128.1 %all-gather.6.cloned.1.call-done = bf16[4096,3072]{1,0:T(8,128)(2,1)} async-done(((bf16[256,3072]{1,0:T(8,128)(2,1)}), bf16[4096,3072]{1,0:T(8,128)(2,1)}) %all-gather.6.cloned.1.call-update) | async-done | bytes 25165840 | tf_op jit(solution)/shard_map/all_gather | solution.py:52
  175.5 12.7 %fusion.7 = f32[256,3072]{1,0:T(8,128)S(1)} fusion(bf16[4096,3072]{1,0:T(8,128)(2,1)} %all-gather.6.cloned.1.call-done, bf16[256,4096]{1,0:T(8,128)(2,1)} %all-gather.4.cloned.1.call-done, f32[4096]{0:T(1024)S(1)} %convert_element_type.19, f32[256]{0:T(256)S(1)} %add_rsqrt_fusion), kind=kOutput, calls=%fused_computation.14 | convolution fusion | flops 6446645248 | bytes 30426112 | tf_op jit(solution)/shard_map/dot_general | solution.py:42
  188.3 2.3 copy.13
  190.6 2.4 multiply_subtract_fusion
  193.0 1.2 pad_maximum_fusion
  194.2 2.6 copy.14
  196.8 3.1 select_convert_fusion
  199.9 263.9 %all-gather.8.cloned.1.call-done = bf16[4096,7168]{1,0:T(8,128)(2,1)} async-done(((bf16[256,7168]{1,0:T(8,128)(2,1)}), bf16[4096,7168]{1,0:T(8,128)(2,1)}) %all-gather.8.cloned.1.call-update) | async-done | bytes 58720272 | tf_op jit(solution)/shard_map/all_gather | solution.py:54
  463.7 28.3 %fusion.5 = f32[256,7168]{1,0:T(8,128)} fusion(bf16[4096,7168]{1,0:T(8,128)(2,1)} %all-gather.8.cloned.1.call-done, bf16[256,4096]{1,0:T(8,128)(2,1)} %all-gather.4.cloned.1.call-done, f32[4096]{0:T(1024)S(1)} %convert_element_type.19, f32[256]{0:T(256)S(1)} %add_rsqrt_fusion), kind=kOutput, calls=%fused_computation.13 | convolution fusion | flops 15036579840 | bytes 68174848 | tf_op jit(solution)/shard_map/dot_general | solution.py:42
  492.0 10.2 %reshape.77 = f32[256,2,3584]{2,1,0:T(2,128)} reshape(f32[256,7168]{1,0:T(8,128)} %fusion.5) | data formatting | bytes 14680064 | tf_op jit(solution)/shard_map/reshape | solution.py:57
  502.2 8.0 %fusion.9 = (f32[256,1,3584]{2,1,0:T(1,128)S(1)}, f32[256,1,3584]{2,1,0:T(1,128)S(1)}) fusion(f32[256,2,3584]{2,1,0:T(2,128)} %reshape.77), kind=kLoop, calls=%fused_computation.20 | loop fusion | bytes 14680064 | tf_op jit(solution)/shard_map/slice | solution.py:58
  510.2 2.3 fusion.4
  (9 shorter events, 0.0 us)
Async XLA Ops:
  7.2 2.2 copy-start
  7.2 7.5 %copy-start.1 = (s32[256]{0:T(256)S(1)}, s32[256]{0:T(256)}, u32[]{:S(2)}) copy-start(s32[256]{0:T(256)} %param.5) | copy-start | bytes 3076
  7.2 38.2 %all-gather.4.cloned.1.call-start = ((), (), s32[]{:S(2)}) async-start(), calls=%async_computation | async-start | bytes 3145728 | tf_op jit(solution)/shard_map/all_gather | solution.py:47
  7.9 167.6 %all-gather.6.cloned.1.call-start = ((), (), s32[]{:S(2)}) async-start(), calls=%async_computation.1 | async-start | bytes 26738688 | tf_op jit(solution)/shard_map/all_gather | solution.py:52
  8.7 455.1 %all-gather.8.cloned.1.call-start = ((), (), s32[]{:S(2)}) async-start(), calls=%async_computation.2 | async-start | bytes 62390272 | tf_op jit(solution)/shard_map/all_gather | solution.py:54
Sparse Core Ops, SparseCore 0:
  9.5 35.8 all-gather.3
  47.0 128.5 all-gather.5
  177.1 286.5 all-gather.7
where the time goes:
time: 520 us; the launch traced here: 519 us
  waiting for transfers between devices  424 us (82%)
  matrix products  41 us (8%)
  local copies, waits for them, and re-layouts  23.2 us (4%)
  between operations  13.8 us (3%)
  other arithmetic  11.4 us (2%)
  blocking collectives  5.29 us (1%)
    all_gather x1, waiting for transfers between devices, per_device(): lax.all_gather(gate_up_weight, 'rep', axis=0, tiled=True)  264 us
    all_gather x1, waiting for transfers between devices, per_device(): lax.all_gather(qkv_weight, 'rep', axis=0, tiled=True)  128 us
    dot_general x2, matrix products, contract_rows(): return jnp.dot(chosen, piece, preferred_element_type=jnp.float32)  41 us
    all_gather x1, waiting for transfers between devices, per_device(): lax.all_gather(activations, 'tp', axis=1, tiled=True)  30.2 us
  transfers between devices with their start and end apart: 3, of which 3 were waited for; matrix products, arithmetic and copies ran while one was open for 5% of the time, Pallas kernels for 0%

commit v1 on v0

--- a/solution.py
+++ b/solution.py
@@ -1,12 +1,18 @@
+import functools
+
 import jax
 import jax.numpy as jnp
 from jax import lax
+from jax.experimental import pallas as pl
+from jax.experimental.pallas import tpu as pltpu
 from jax.sharding import PartitionSpec as P
 
 QH = 32
 KVH = 8
 HD = 128
-
+MESH = pl.DeviceIdType.MESH
+CORES = 2
+QUARTERS = 4
 
 theta_base = 500000.0
 norm_eps = 1e-05
@@ -20,15 +26,21 @@
     )
 
 
+def angle_parts(positions):
+    half_size = HD // 2
+    frequency = theta_base ** (-2.0 * jnp.arange(half_size, dtype=jnp.float32) / HD)
+    angles = positions.astype(jnp.float32)[:, None] * frequency[None, :]
+    return jnp.cos(angles), jnp.sin(angles)
+
+
 def rotary(joined_qkv, positions):
     row_count = joined_qkv.shape[0]
     per_group = QH // KVH + 2
     half_size = HD // 2
     head_view = joined_qkv.reshape(row_count, -1, per_group, HD)
-    frequency = theta_base ** (-2.0 * jnp.arange(half_size, dtype=jnp.float32) / HD)
-    angles = positions.astype(jnp.float32)[:, None] * frequency[None, :]
-    cosine = jnp.cos(angles)[:, None, None, :]
-    sine_part = jnp.sin(angles)[:, None, None, :]
+    cosine, sine_part = angle_parts(positions)
+    cosine = cosine[:, None, None, :]
+    sine_part = sine_part[:, None, None, :]
     leading = head_view[..., :half_size]
     trailing = head_view[..., half_size:]
     turned = jnp.concatenate(
@@ -42,7 +54,7 @@
     return jnp.dot(chosen, piece, preferred_element_type=jnp.float32)
 
 
-def per_device(positions, activations, norm_gain, qkv_weight, gate_up_weight):
+def plain(positions, activations, norm_gain, qkv_weight, gate_up_weight):
     features, gains = (
         lax.all_gather(activations, "tp", axis=1, tiled=True),
         lax.all_gather(norm_gain, "tp", axis=0, tiled=True),
@@ -59,10 +71,319 @@
     return (qkv_out, hidden)
 
 
+def widths_of(total):
+    widths = [256] * (total // 256)
+    return widths + ([total % 256] if total % 256 else [])
+
+
+def kernel(plan, table_in, x_in, gain_in, wq_in, wg_in, q_out, h_out, *scratch):
+    (chips, seqs, feats, qcols, hcols, widths) = plan
+    n_gu = len(widths)
+    x_buf, t_buf, g_buf, q_res, wq_buf = scratch[:5]
+    gu_bufs = scratch[5 : 5 + n_gu]
+    h_res = scratch[5 + n_gu : 5 + 2 * n_gu]
+    (w_send, w_recv, f_send, f_recv, o_send, o_recv, a_send, a_recv, l_sem) = scratch[5 + 2 * n_gu :]
+
+    rep, t = lax.axis_index("rep"), lax.axis_index("tp")
+    core = rep % CORES
+    chip = rep // CORES
+    half = chip // QUARTERS
+    quarter = chip % QUARTERS
+    zl, y = quarter // 2, quarter % 2
+
+    def dev(other_chip, other_core=None, other_t=None):
+        return (
+            other_chip * CORES + (core if other_core is None else other_core),
+            t if other_t is None else other_t,
+        )
+
+    sibling = dev(chip, 1 - core)
+    across = dev(chip, core, 1 - t)
+    z_peer = dev(half * QUARTERS + (1 - zl) * 2 + y)
+    y_peer = dev(half * QUARTERS + zl * 2 + (1 - y))
+
+    barrier = pltpu.get_barrier_semaphore()
+    for k in range(1, chips):
+        pl.semaphore_signal(barrier, inc=1, device_id=dev((chip + k) % chips), device_id_type=MESH)
+    pl.semaphore_signal(barrier, inc=1, device_id=sibling, device_id_type=MESH)
+    pl.semaphore_signal(barrier, inc=1, device_id=across, device_id_type=MESH)
+    pl.semaphore_wait(barrier, chips + 1)
+
+    def remote(src, dst, ssem, rsem, where):
+        return pltpu.make_async_remote_copy(
+            src_ref=src, dst_ref=dst, send_sem=ssem, recv_sem=rsem, device_id=where, device_id_type=MESH
+        )
+
+    def rows(index, count=1):
+        return pl.ds(pl.multiple_of(index * seqs, seqs), count * seqs)
+
+    def cols(base, width):
+        return pl.ds(pl.multiple_of(base, HD), width)
+
+    slot = y * 2 + zl
+    mine = cols(t * feats, feats)
+    theirs = cols((1 - t) * feats, feats)
+    local = [
+        pltpu.make_async_copy(x_in, x_buf.at[rows(slot), mine], l_sem.at[0]),
+        pltpu.make_async_copy(table_in, t_buf.at[rows(slot)], l_sem.at[1]),
+        pltpu.make_async_copy(gain_in, g_buf.at[:, mine], l_sem.at[2]),
+    ]
+    other = y * 2 + (1 - zl)
+    z_x = remote(x_in, x_buf.at[rows(slot), mine], a_send.at[0], a_recv.at[0], z_peer)
+    z_t = remote(table_in, t_buf.at[rows(slot)], a_send.at[1], a_recv.at[1], z_peer)
+    x_own = remote(x_in, x_buf.at[rows(slot), mine], a_send.at[2], a_recv.at[2], across)
+    x_gain = remote(gain_in, g_buf.at[:, mine], a_send.at[3], a_recv.at[3], across)
+    y_own = remote(x_in, x_buf.at[rows(slot), mine], a_send.at[4], a_recv.at[4], y_peer)
+    y_t = remote(table_in, t_buf.at[rows(slot)], a_send.at[5], a_recv.at[5], y_peer)
+    y_two = remote(x_buf.at[rows(other), mine], x_buf.at[rows(other), mine], a_send.at[6], a_recv.at[6], y_peer)
+    y_t2 = remote(t_buf.at[rows(other)], t_buf.at[rows(other)], a_send.at[7], a_recv.at[7], y_peer)
+    x_two = remote(x_buf.at[rows(other), mine], x_buf.at[rows(other), mine], a_send.at[8], a_recv.at[8], across)
+    far = (1 - y) * 2 + zl
+    far2 = (1 - y) * 2 + (1 - zl)
+    x_three = remote(x_buf.at[rows(far), mine], x_buf.at[rows(far), mine], a_send.at[9], a_recv.at[9], across)
+    x_four = remote(x_buf.at[rows(far2), mine], x_buf.at[rows(far2), mine], a_send.at[10], a_recv.at[10], across)
+
+    pieces = [(wq_in, lambda q: q * qcols, qcols, wq_buf, 0)]
+    chunks = [[0]]
+    at = 0
+    for n, width in enumerate(widths):
+        for part in range(2):
+            base = part * hcols * QUARTERS + at
+            pieces.append((wg_in, lambda q, base=base: base + q * hcols, width, gu_bufs[n], part * width))
+        chunks.append([2 * n + 1, 2 * n + 2])
+        at += width
+
+    def piece_src(p, q):
+        src, col, width, _, _ = pieces[p]
+        return src.at[:, cols(col(q), width)]
+
+    def piece_dst(p, owner_rep):
+        _, _, width, buf, col = pieces[p]
+        return buf.at[rows(owner_rep), col : col + width]
+
+    order = [(k + chips // 2) % chips for k in range(chips)]
+    order = [k for k in order if k]
+
+    def weight_send(p, k):
+        to = (chip + k) % chips
+        return remote(
+            piece_src(p, to % QUARTERS), piece_dst(p, rep), w_send.at[p, k], w_recv.at[p, chip], dev(to)
+        )
+
+    def weight_from(p, k):
+        source = (chip + chips - k) % chips
+        owner = source * CORES + core
+        return remote(
+            piece_dst(p, owner), piece_dst(p, owner), w_send.at[p, k], w_recv.at[p, source], dev(source)
+        )
+
+    def own_local(p):
+        return pltpu.make_async_copy(piece_src(p, quarter), piece_dst(p, rep), l_sem.at[3 + p])
+
+    def own_pass(p):
+        return remote(piece_src(p, quarter), piece_dst(p, rep), f_send.at[p, 0], f_recv.at[p, 0], sibling)
+
+    def passed(p, k):
+        source = (chip + chips - k) % chips
+        owner = source * CORES + core
+        return remote(piece_dst(p, owner), piece_dst(p, owner), f_send.at[p, k], f_recv.at[p, k], sibling)
+
+    def passed_in(p, k):
+        source = (chip + chips - k) % chips
+        owner = source * CORES + (1 - core)
+        return remote(piece_dst(p, owner), piece_dst(p, owner), f_send.at[p, k], f_recv.at[p, k], sibling)
+
+    def start_chunk(c):
+        for k in order:
+            for p in chunks[c]:
+                weight_send(p, k).start()
+        for p in chunks[c]:
+            own_local(p).start()
+            own_pass(p).start()
+
+    def pass_chunk(c):
+        for k in order:
+            for p in chunks[c]:
+                weight_from(p, k).wait_recv()
+                passed(p, k).start()
+
+    def finish_chunk(c):
+        for p in chunks[c]:
+            own_local(p).wait()
+            for k in range(chips):
+                passed_in(p, k).wait_recv()
+
+    for copy in (z_x, z_t, x_own, x_gain, y_own, y_t, *local):
+        copy.start()
+    start_chunk(0)
+    z_x.wait_recv()
+    y_two.start()
+    x_two.start()
+    z_t.wait_recv()
+    y_t2.start()
+    for c in range(1, len(chunks)):
+        start_chunk(c)
+    y_own.wait_recv()
+    x_three.start()
+    y_two.wait_recv()
+    x_four.start()
+    pass_chunk(0)
+    for copy in (y_t, y_t2, x_own, x_gain, x_two, x_three, x_four):
+        copy.wait_recv()
+    for copy in local:
+        copy.wait()
+    for copy in (z_x, z_t, x_own, x_gain, y_own, y_t, y_two, y_t2, x_two, x_three, x_four):
+        copy.wait_send()
+
+    total = QUARTERS * seqs
+    tall = 32
+
+    @pl.loop(0, total // tall)
+    def _(i):
+        at_rows = pl.ds(pl.multiple_of(i * tall, tall), tall)
+        values = x_buf[at_rows, :].astype(jnp.float32)
+        mean_square = jnp.mean(values * values, axis=1, keepdims=True)
+        x_buf[at_rows, :] = (values * lax.rsqrt(mean_square + norm_eps) * g_buf[...]).astype(jnp.bfloat16)
+
+    per_group = QH // KVH + 2
+    deep = 2 * seqs
+
+    def compute(c):
+        @pl.loop(0, total // deep)
+        def _(i):
+            at_rows = pl.ds(pl.multiple_of(i * deep, deep), deep)
+            chosen = x_buf[at_rows, :]
+            if c == 0:
+                table = t_buf[at_rows, :]
+                swapped = pltpu.roll(table, HD // 2, 1)
+                lane = lax.broadcasted_iota(jnp.int32, table.shape, 1)
+                low = lane < HD // 2
+                cosine = jnp.where(low, table, swapped)
+                sine_part = jnp.where(low, -swapped, table)
+                for n in range(0, qcols, 2 * HD):
+                    wide = jnp.dot(chosen, wq_buf[:, n : n + 2 * HD], preferred_element_type=jnp.float32)
+                    for s in range(2):
+                        head = wide[:, s * HD : (s + 1) * HD]
+                        if (n // HD + s) % per_group < per_group - 1:
+                            head = head * cosine + pltpu.roll(head, HD // 2, 1) * sine_part
+                        q_res[at_rows, n + s * HD : n + (s + 1) * HD] = head.astype(jnp.bfloat16)
+            else:
+                width = widths[c - 1]
+                both = jnp.dot(chosen, gu_bufs[c - 1][...], preferred_element_type=jnp.float32)
+                gate, up = both[:, :width], both[:, width:]
+                h_res[c - 1][at_rows, :] = (gate / (1.0 + jnp.exp(-gate)) * up).astype(jnp.bfloat16)
+
+    def result(c, q):
+        place = (q % 2) * 2 + q // 2
+        if c == 0:
+            return q_res.at[rows(place)], lambda mover: q_out.at[:, cols(mover * qcols, qcols)]
+        offset = sum(widths[: c - 1])
+        return h_res[c - 1].at[rows(place)], lambda mover: h_out.at[:, cols(mover * hcols + offset, widths[c - 1])]
+
+    def out_send(c, k):
+        to = (quarter + k) % QUARTERS
+        src, dst = result(c, to)
+        return remote(src, dst(quarter), o_send.at[c, k], o_recv.at[c, k], dev(half * QUARTERS + to))
+
+    def out_from(c, k):
+        source = (quarter + QUARTERS - k) % QUARTERS
+        src, dst = result(c, quarter)
+        return remote(src, dst(source), o_send.at[c, k], o_recv.at[c, k], dev(half * QUARTERS + source))
+
+    def out_local(c):
+        src, dst = result(c, quarter)
+        return pltpu.make_async_copy(src, dst(quarter), l_sem.at[3 + len(pieces) + c])
+
+    def ship(c):
+        for k in range(1, QUARTERS):
+            out_send(c, k).start()
+        out_local(c).start()
+
+    for c in range(len(chunks)):
+        if c + 1 < len(chunks):
+            pass_chunk(c + 1)
+        finish_chunk(c)
+        compute(c)
+        ship(c)
+
+    for c in range(len(chunks)):
+        for p in chunks[c]:
+            for k in range(1, chips):
+                weight_send(p, k).wait_send()
+                passed(p, k).wait_send()
+            own_pass(p).wait_send()
+        out_local(c).wait()
+        for k in range(1, QUARTERS):
+            out_send(c, k).wait_send()
+            out_from(c, k).wait_recv()
+
+
+def fused(chips, positions, activations, norm_gain, qkv_weight, gate_up_weight):
+    seqs, feats = activations.shape
+    depth, qkv_cols = qkv_weight.shape
+    qcols = qkv_cols // QUARTERS
+    hcols = gate_up_weight.shape[1] // 2 // QUARTERS
+    widths = widths_of(hcols)
+    rank = chips * CORES
+    table = jnp.concatenate(angle_parts(positions), axis=1)
+    gains = norm_gain.astype(jnp.float32)[None, :]
+    bf16, f32 = jnp.bfloat16, jnp.float32
+    pieces, chunks = 1 + 2 * len(widths), 1 + len(widths)
+    dma = pltpu.SemaphoreType.DMA
+    scratch = [
+        pltpu.VMEM((QUARTERS * seqs, 2 * feats), bf16),
+        pltpu.VMEM((QUARTERS * seqs, HD), f32),
+        pltpu.VMEM((1, 2 * feats), f32),
+        pltpu.VMEM((QUARTERS * seqs, qcols), bf16),
+        pltpu.VMEM((rank * depth, qcols), bf16),
+        *[pltpu.VMEM((rank * depth, 2 * w), bf16) for w in widths],
+        *[pltpu.VMEM((QUARTERS * seqs, w), bf16) for w in widths],
+        dma((pieces, chips)),
+        dma((pieces, chips)),
+        dma((pieces, chips)),
+        dma((pieces, chips)),
+        dma((chunks, QUARTERS)),
+        dma((chunks, QUARTERS)),
+        dma((11,)),
+        dma((11,)),
+        dma((3 + pieces + chunks,)),
+    ]
+    plan = (chips, seqs, feats, qcols, hcols, tuple(widths))
+    anywhere = pl.BlockSpec(memory_space=pl.ANY)
+    return pl.pallas_call(
+        functools.partial(kernel, plan),
+        out_shape=(
+            jax.ShapeDtypeStruct((seqs, qkv_cols), bf16),
+            jax.ShapeDtypeStruct((seqs, hcols * QUARTERS), bf16),
+        ),
+        in_specs=[anywhere] * 5,
+        out_specs=(anywhere, anywhere),
+        scratch_shapes=scratch,
+        compiler_params=pltpu.CompilerParams(
+            collective_id=0, has_side_effects=True, vmem_limit_bytes=60 * 1024 * 1024
+        ),
+    )(table, activations, gains, qkv_weight, gate_up_weight)
+
+
+def per_device(reps, tps, positions, activations, norm_gain, qkv_weight, gate_up_weight):
+    chips = reps // CORES
+    seqs, depth = activations.shape[0], qkv_weight.shape[0]
+    fits = (
+        chips == 2 * QUARTERS
+        and tps == 2
+        and seqs == depth
+        and seqs % 32 == 0
+        and qkv_weight.shape[1] % (QUARTERS * (QH // KVH + 2) * HD) == 0
+        and gate_up_weight.shape[1] % (2 * QUARTERS * HD) == 0
+    )
+    step = functools.partial(fused, chips) if fits else plain
+    return step(positions, activations, norm_gain, qkv_weight, gate_up_weight)
+
+
 def solution(mesh):
     placed = (P("rep"), P("rep", "tp"), P("tp"), P("rep", "tp"), P("rep", "tp"))
     return jax.shard_map(
-        per_device,
+        functools.partial(per_device, mesh.shape["rep"], mesh.shape["tp"]),
         mesh=mesh,
         in_specs=placed,
         out_specs=(P("rep", "tp"), P("rep", "tp")),

time: 520 us -> 261 us (0.50)
  waiting for transfers between devices: 424 us -> 0 us
  Pallas kernels: 0 us -> 253 us
  matrix products: 41 us -> 0 us
  local copies, waits for them, and re-layouts: 23.2 us -> 4.02 us
  between operations: 13.8 us -> 0.66 us
  other arithmetic: 11.4 us -> 3.27 us
  blocking collectives: 5.29 us -> 0 us
    all_gather x3 -> x0, waiting for transfers between devices: 422 us -> none  [the longest x1 264 us: per_device(): lax.all_gather(gate_up_weight, 'rep', axis=0, tiled=True)]
    pallas_call x0 -> x1, Pallas kernels: none -> 253 us  [fused(): pl.pallas_call(functools.partial(kernel, plan), out_shape=(jax.ShapeDtype...]
    dot_general x2 -> x0, matrix products: 41 us -> none  [contract_rows(): return jnp.dot(chosen, piece, preferred_element_type=jnp.float32)]
    reshape x1 -> x0, local copies, waits for them, and re-layouts: 10.2 us -> none  [per_device(): paired = gateup_partial.reshape(seq_count, 2, -1)]
    slice x1 -> x0, local copies, waits for them, and re-layouts: 8 us -> none  [per_device(): hidden = (jax.nn.silu(paired[:, 0]) * paired[:, 1]).astype(jnp.bfloat16)]
    all_gather x1 -> x0, blocking collectives: 5.29 us -> none  [per_device(): lax.all_gather(norm_gain, 'tp', axis=0, tiled=True)]
  transfers between devices with their start and end apart: 3 -> 0, of which waited for: 3 -> 0; matrix products, arithmetic and copies ran while one was open for 5% -> 0% of each run, Pallas kernels for 0% -> 0%
where the time goes in v1:
time: 261 us
  Pallas kernels  253 us (97%)
  local copies, waits for them, and re-layouts  4.02 us (2%)
  other arithmetic  3.27 us (1%)
    pallas_call x1, Pallas kernels, fused(): pl.pallas_call(functools.partial(kernel, plan), out_shape=(jax.ShapeDtype...  253 us

profile of v1, /device:TPU:0, one launch (start us, length us, event | category | flops | bytes accessed | tf_op | source)
XLA Modules:
  0.0 260.9 jit_solution(12069862918654866722)
XLA Ops:
  0.6 0.7 convert_element_type.4
  1.3 1.3 broadcast_in_dim.9
  2.6 0.5 multiply_cosine_fusion
  3.1 0.8 pad_maximum_fusion.table_in
  3.9 252.9 %shard_map.68 = (bf16[256,3072]{1,0:T(8,128)(2,1)}, bf16[256,3584]{1,0:T(8,128)(2,1)}) custom-call(f32[256,128]{1,0:T(8,128)} %pad_maximum_fusion.table_in, bf16[256,2048]{1,0:T(8,128)(2,1)} %x_in.1, f32[1,2048]{1,0:T(1,128)} %bitcast.1, bf16[256,3072]{1,0:T(8,128)(2,1)} %wq_in.1, bf16[256,7168]{1,0:T(8,128)(2,1)} %wg_in.1), custom_call_target="tpu_custom_call" | custom-call | tf_op jit(solution)/shard_map/pallas_call | solution.py:353
  256.9 0.0 copy-start
  256.9 2.8 %copy.9 = bf16[256,3072]{1,0:T(8,128)(2,1)} copy(bf16[256,3072]{1,0:T(8,128)(2,1)} %get-tuple-element.6) | data formatting | bytes 3145728
  259.7 0.0 copy-done
  259.7 1.2 copy.10
  (1 shorter events, 0.0 us)
Async XLA Ops:
  256.9 2.8 %copy-start = (bf16[256,3584]{1,0:T(8,128)(2,1)S(1)}, bf16[256,3584]{1,0:T(8,128)(2,1)}, u32[]{:S(2)}) copy-start(bf16[256,3584]{1,0:T(8,128)(2,1)} %get-tuple-element.7) | copy-start | bytes 5505028

commit v2 on v1

--- a/solution.py
+++ b/solution.py
@@ -126,13 +126,13 @@
     local = [
         pltpu.make_async_copy(x_in, x_buf.at[rows(slot), mine], l_sem.at[0]),
         pltpu.make_async_copy(table_in, t_buf.at[rows(slot)], l_sem.at[1]),
-        pltpu.make_async_copy(gain_in, g_buf.at[:, mine], l_sem.at[2]),
+        pltpu.make_async_copy(gain_in, g_buf.at[mine], l_sem.at[2]),
     ]
     other = y * 2 + (1 - zl)
     z_x = remote(x_in, x_buf.at[rows(slot), mine], a_send.at[0], a_recv.at[0], z_peer)
     z_t = remote(table_in, t_buf.at[rows(slot)], a_send.at[1], a_recv.at[1], z_peer)
     x_own = remote(x_in, x_buf.at[rows(slot), mine], a_send.at[2], a_recv.at[2], across)
-    x_gain = remote(gain_in, g_buf.at[:, mine], a_send.at[3], a_recv.at[3], across)
+    x_gain = remote(gain_in, g_buf.at[mine], a_send.at[3], a_recv.at[3], across)
     y_own = remote(x_in, x_buf.at[rows(slot), mine], a_send.at[4], a_recv.at[4], y_peer)
     y_t = remote(table_in, t_buf.at[rows(slot)], a_send.at[5], a_recv.at[5], y_peer)
     y_two = remote(x_buf.at[rows(other), mine], x_buf.at[rows(other), mine], a_send.at[6], a_recv.at[6], y_peer)
@@ -238,12 +238,14 @@
     total = QUARTERS * seqs
     tall = 32
 
+    gain_row = g_buf[...].astype(jnp.float32)[None, :]
+
     @pl.loop(0, total // tall)
     def _(i):
         at_rows = pl.ds(pl.multiple_of(i * tall, tall), tall)
         values = x_buf[at_rows, :].astype(jnp.float32)
         mean_square = jnp.mean(values * values, axis=1, keepdims=True)
-        x_buf[at_rows, :] = (values * lax.rsqrt(mean_square + norm_eps) * g_buf[...]).astype(jnp.bfloat16)
+        x_buf[at_rows, :] = (values * lax.rsqrt(mean_square + norm_eps) * gain_row).astype(jnp.bfloat16)
 
     per_group = QH // KVH + 2
     deep = 2 * seqs
@@ -300,11 +302,13 @@
         out_local(c).start()
 
     for c in range(len(chunks)):
-        if c + 1 < len(chunks):
-            pass_chunk(c + 1)
+        if c:
+            pass_chunk(c)
         finish_chunk(c)
         compute(c)
         ship(c)
+        if c + 99 < len(chunks):
+            start_chunk(c + 99)
 
     for c in range(len(chunks)):
         for p in chunks[c]:
@@ -326,14 +330,14 @@
     widths = widths_of(hcols)
     rank = chips * CORES
     table = jnp.concatenate(angle_parts(positions), axis=1)
-    gains = norm_gain.astype(jnp.float32)[None, :]
+    gains = norm_gain
     bf16, f32 = jnp.bfloat16, jnp.float32
     pieces, chunks = 1 + 2 * len(widths), 1 + len(widths)
     dma = pltpu.SemaphoreType.DMA
     scratch = [
         pltpu.VMEM((QUARTERS * seqs, 2 * feats), bf16),
         pltpu.VMEM((QUARTERS * seqs, HD), f32),
-        pltpu.VMEM((1, 2 * feats), f32),
+        pltpu.VMEM((2 * feats,), bf16),
         pltpu.VMEM((QUARTERS * seqs, qcols), bf16),
         pltpu.VMEM((rank * depth, qcols), bf16),
         *[pltpu.VMEM((rank * depth, 2 * w), bf16) for w in widths],
@@ -353,11 +357,11 @@
     return pl.pallas_call(
         functools.partial(kernel, plan),
         out_shape=(
-            jax.ShapeDtypeStruct((seqs, qkv_cols), bf16),
-            jax.ShapeDtypeStruct((seqs, hcols * QUARTERS), bf16),
+            pltpu.VMEM((seqs, qkv_cols), bf16),
+            pltpu.VMEM((seqs, hcols * QUARTERS), bf16),
         ),
         in_specs=[anywhere] * 5,
-        out_specs=(anywhere, anywhere),
+        out_specs=(pl.BlockSpec(memory_space=pltpu.VMEM), pl.BlockSpec(memory_space=pltpu.VMEM)),
         scratch_shapes=scratch,
         compiler_params=pltpu.CompilerParams(
             collective_id=0, has_side_effects=True, vmem_limit_bytes=60 * 1024 * 1024

time: 261 us -> 252 us (0.966)
  Pallas kernels: 253 us -> 246 us
    pallas_call x1, Pallas kernels: 253 us -> 246 us  [fused(): pl.pallas_call(functools.partial(kernel, plan), out_shape=(pltpu.VMEM((se...]
where the time goes in v2:
time: 252 us; the launch traced here: 251 us
  Pallas kernels  246 us (98%)
    pallas_call x1, Pallas kernels, fused(): pl.pallas_call(functools.partial(kernel, plan), out_shape=(pltpu.VMEM((se...  246 us

profile of v2, /device:TPU:0, one launch (start us, length us, event | category | flops | bytes accessed | tf_op | source)
XLA Modules:
  0.0 251.0 jit_solution(8470249350605172467)
XLA Ops:
  0.6 0.7 convert_element_type.3
  1.3 0.5 multiply_cosine_fusion
  1.9 0.8 pad_maximum_fusion.table_in
  2.6 246.0 %shard_map.68 = (bf16[256,3072]{1,0:T(8,128)(2,1)S(1)}, bf16[256,3584]{1,0:T(8,128)(2,1)S(1)}) custom-call(f32[256,128]{1,0:T(8,128)} %pad_maximum_fusion.table_in, bf16[256,2048]{1,0:T(8,128)(2,1)} %x_in.1, bf16[2048]{0:T(1024)(128)(2,1)} %gain_in.1, bf16[256,3072]{1,0:T(8,128)(2,1)} %wq_in.1, bf16[256,7168]{1,0:T(8,128)(2,1)} %wg_in.1), custom_call_target="tpu_custom_call" | custom-call | tf_op jit(solution)/shard_map/pallas_call | solution.py:357
  248.6 1.1 copy.9
  249.7 1.2 copy.10
  (1 shorter events, 0.0 us)

commit v3 on v2

--- a/solution.py
+++ b/solution.py
@@ -72,8 +72,10 @@
 
 
 def widths_of(total):
-    widths = [256] * (total // 256)
-    return widths + ([total % 256] if total % 256 else [])
+    blocks = total // HD
+    tail = min(3, blocks)
+    wide, left = divmod(blocks - tail, QUARTERS)
+    return [QUARTERS * HD] * wide + ([left * HD] if left else []) + [HD] * tail
 
 
 def kernel(plan, table_in, x_in, gain_in, wq_in, wg_in, q_out, h_out, *scratch):

time: 252 us -> 250 us (level)
  no operation moved by 1% of the time
where the time goes in v3:
time: 250 us; the launch traced here: 249 us
  Pallas kernels  244 us (98%)
    pallas_call x1, Pallas kernels, fused(): pl.pallas_call(functools.partial(kernel, plan), out_shape=(pltpu.VMEM((se...  244 us

profile of v3, /device:TPU:0, one launch (start us, length us, event | category | flops | bytes accessed | tf_op | source)
XLA Modules:
  0.0 249.0 jit_solution(15624929625030205682)
XLA Ops:
  0.6 0.7 convert_element_type.3
  1.3 0.5 multiply_cosine_fusion
  1.9 0.8 pad_maximum_fusion.table_in
  2.6 243.9 %shard_map.68 = (bf16[256,3072]{1,0:T(8,128)(2,1)S(1)}, bf16[256,3584]{1,0:T(8,128)(2,1)S(1)}) custom-call(f32[256,128]{1,0:T(8,128)} %pad_maximum_fusion.table_in, bf16[256,2048]{1,0:T(8,128)(2,1)} %x_in.1, bf16[2048]{0:T(1024)(128)(2,1)} %gain_in.1, bf16[256,3072]{1,0:T(8,128)(2,1)} %wq_in.1, bf16[256,7168]{1,0:T(8,128)(2,1)} %wg_in.1), custom_call_target="tpu_custom_call" | custom-call | tf_op jit(solution)/shard_map/pallas_call | solution.py:359
  246.6 1.1 copy.9
  247.7 1.2 copy.10
  (1 shorter events, 0.0 us)
